TPU v7x, 32 devices: a whole 2x2x4 slice. The times are simulated.
32 devices in a mesh: groups: 2 (over y), expert: 8 (over z, x), sub: 2 (over core).
Axes of the slice: x: 2, y: 2, z: 4, core: 2. Of those that a mesh axis runs over, the one named last changes fastest.
Arguments:
- stream_in: bfloat16 [1024, 3072], P(('groups', 'expert'), 'sub'), parts along dimension 0, may hold values from -0.29882812 to 0.29882812
- queries: bfloat16 [1024, 3072], P(('groups', 'expert'), 'sub'), parts along dimension 0, may hold values from -6 to 6
- kv_new: bfloat16 [2, 1024, 1024], P(None, ('groups', 'expert'), 'sub'), parts along dimension 1, may hold values from -6 to 6
- paged_key_value_cache: bfloat16 [2, 32, 4, 1024], P(None, ('groups', 'expert'), None, 'sub'), parts along dimension 1, may hold values from -6 to 6
- page_table: int32 [16, 8], P(('groups', 'expert')), parts along dimension 0, may hold values from 0 to 15, as said below
- prefix_len: int32 [16], P(('groups', 'expert')), parts along dimension 0, may hold values from 8 to 32
- norm_gain: float32 [3072], replicated, may hold values from 0.5 to 1.5
- w_router: bfloat16 [3072, 8], replicated, may hold values from -0.21875 to 0.21875
- expert_ids: int32 [1024, 2], P(('groups', 'expert')), parts along dimension 0, may hold values from 0 to 7, as said below
- w_in: bfloat16 [2, 3072, 65536], P(None, None, ('expert', 'sub')), may hold values from -0.109375 to 0.109375
Outputs:
- stream: bfloat16 [1024, 3072], P(('groups', 'expert'), 'sub'), parts along dimension 0
- expert_hidden: bfloat16 [272, 65536], P('groups', ('expert', 'sub')), parts along dimension 0
There are 2 independent parts, one for each index of `groups`. A program takes and returns all parts, laid end to end along the dimension named above; an argument that names none is the same for every part. Nothing has to cross between parts.
Inputs may be any that keep to these rules, and one draw needn't show every extreme that they name: `expert_ids`: each row names two different experts. The rows of one request name each expert at most 17 times, and one expert is named exactly 17 times by the rows of every request. `page_table`: the pages of one row lie in different shards: page // 2 differs along a row. Requests share leading pages.
All inputs are finite; a program needn't handle non-finite values.
Results may differ from a plain program's by a relative error of at most 0.018.
Values may be sent and summed in bfloat16 or wider, within the bound.
A program may use at most 128 MiB of HBM per device.

v0:
```python
import math

import jax
import jax.numpy as jnp
from jax import lax
from jax.sharding import PartitionSpec as P

HEAD_WIDTH = 128
EXPERTS = 8
TOP = 2
CAP = 17


def for_sending(array):

    def short(part):
        return part.astype(jnp.bfloat16) if part.dtype == jnp.float32 else part

    return jax.tree.map(short, array)


def partner(array, axis, apart):
    return lax.ppermute(array, axis, [(i, i ^ 1 << apart) for i in range(lax.axis_size(axis))])


def from_behind(value, axis, steps):
    count = lax.axis_size(axis)
    pairs = [(source, (source + steps) % count) for source in range(count)]
    return lax.ppermute(value, axis, pairs)


def attend(query_rows, key_rows, prefix_length, head_size):
    tokens_here = query_rows.shape[0]
    length = key_rows.shape[1]
    kv_heads = key_rows.shape[2] // head_size
    grouped = query_rows.shape[1] // head_size // kv_heads
    query_f = query_rows.reshape(tokens_here, kv_heads, grouped, head_size).astype(jnp.float32)
    keys_f = key_rows[0].reshape(length, kv_heads, head_size).astype(jnp.float32)
    values_f = key_rows[1].reshape(length, kv_heads, head_size).astype(jnp.float32)
    scores = jnp.einsum("tkgd,lkd->kgtl", query_f, keys_f) * (1.0 / math.sqrt(head_size))
    prefix_span = length - tokens_here
    places = jnp.arange(length)[None, :]
    rows_at = jnp.arange(tokens_here)[:, None]
    is_live = jnp.where(
        places < prefix_span, places < prefix_length, places - prefix_span <= rows_at
    )
    scores = jnp.where(is_live, scores, -1e30)
    largest = jnp.max(scores, axis=-1, keepdims=True)
    exponent = jnp.exp(scores - largest)
    weights = (exponent / jnp.sum(exponent, axis=-1, keepdims=True)).astype(jnp.bfloat16)
    mixed_heads = jnp.einsum("kgtl,lkd->tkgd", weights.astype(jnp.float32), values_f)
    return mixed_heads.reshape(tokens_here, -1).astype(jnp.bfloat16)


def pick_block(stack_rows, position):
    return lax.dynamic_index_in_dim(stack_rows, position, 0, keepdims=False)


def spread(kept_rows, kept_shares, own_index, level_values):
    for depth_bit in range(level_values):
        partner_rows, partner_shares = (
            partner(for_sending(kept_rows), "expert", depth_bit).astype(kept_rows.dtype),
            partner(for_sending(kept_shares), "expert", depth_bit).astype(kept_shares.dtype),
        )
        high_bit = (own_index >> depth_bit) % 2 == 1
        lower_rows = jnp.where(high_bit, partner_rows, kept_rows)
        upper_rows = jnp.where(high_bit, kept_rows, partner_rows)
        lower_shares = jnp.where(high_bit, partner_shares, kept_shares)
        upper_shares = jnp.where(high_bit, kept_shares, partner_shares)
        kept_rows = jnp.concatenate([lower_rows, upper_rows], axis=0)
        kept_shares = jnp.concatenate([lower_shares, upper_shares], axis=0)
    return (kept_rows, kept_shares)


def shards(
    stream_in,
    queries,
    kv_new,
    paged_key_value_cache,
    page_table,
    prefix_len,
    norm_gain,
    w_router,
    expert_ids,
    w_in,
):
    expert_count = lax.axis_size("expert")
    group_width = expert_count // EXPERTS
    level_values = group_width.bit_length() - 1
    own_index = lax.axis_index("expert")
    own_group = own_index // group_width
    shard_pages = paged_key_value_cache.shape[1]
    page_list = page_table[0]
    owners = page_list // shard_pages
    inside = page_list % shard_pages
    owner_hot = owners[None, :] == jnp.arange(expert_count, dtype=jnp.int32)[:, None]
    wanted = jnp.sum(jnp.where(owner_hot, inside[None, :], 0), axis=1)
    asked_for = lax.all_to_all(wanted[:, None], "expert", split_axis=0, concat_axis=0, tiled=True)
    served = jnp.take(paged_key_value_cache, asked_for[:, 0], axis=1)
    arrived = lax.all_to_all(served, "expert", split_axis=1, concat_axis=1, tiled=True)
    prefix_pages = jnp.take(arrived, owners, axis=1)
    prefix_row_block = prefix_pages.reshape(2, -1, prefix_pages.shape[-1])
    key_rows = jnp.concatenate([prefix_row_block, kv_new], axis=1)
    attended = attend(queries, key_rows, prefix_len[0], HEAD_WIDTH)
    stream_part = (stream_in.astype(jnp.float32) + attended.astype(jnp.float32)).astype(
        jnp.bfloat16
    )
    stream = lax.all_gather(stream_part, "sub", axis=1, tiled=True)
    stream_f = stream.astype(jnp.float32)
    scale_rows = lax.rsqrt(jnp.mean(stream_f * stream_f, axis=-1, keepdims=True) + 1e-05)
    normed = (stream_f * scale_rows * norm_gain).astype(jnp.bfloat16)
    logits = jnp.dot(normed, w_router, preferred_element_type=jnp.float32)
    chosen = jnp.take_along_axis(logits, expert_ids, axis=1)
    gate_share = jax.nn.sigmoid(chosen - chosen[:, ::-1])
    row_count = stream_in.shape[0]
    routes = expert_ids.reshape(-1)
    route_count = routes.shape[0]
    expert_hot = (routes[:, None] == jnp.arange(EXPERTS, dtype=jnp.int32)[None, :]).astype(
        jnp.int32
    )
    route_rank = jnp.sum((jnp.cumsum(expert_hot, axis=0) - 1) * expert_hot, axis=1)
    slot_hot = (route_rank[:, None] == jnp.arange(CAP, dtype=jnp.int32)[None, :]).astype(
        jnp.float32
    )
    row_hot = ((jnp.arange(route_count) // TOP)[:, None] == jnp.arange(row_count)[None, :]).astype(
        jnp.float32
    )
    route_place = expert_hot.astype(jnp.float32)[:, :, None] * slot_hot[:, None, :]
    picker = jnp.einsum("rem,rt->emt", route_place, row_hot)
    shares = jnp.einsum("rem,r->em", route_place, gate_share.reshape(-1))
    outgoing = jnp.einsum(
        "emt,td->emd", picker.astype(jnp.bfloat16), normed, preferred_element_type=jnp.float32
    ).astype(jnp.bfloat16)
    arrived_rows = [pick_block(outgoing, own_group)]
    arrived_shares = [pick_block(shares, own_group)]
    for stride in range(1, EXPERTS):
        target = (own_group + stride) % EXPERTS
        rows_in, shares_in = (
            from_behind(pick_block(outgoing, target), "expert", stride * group_width),
            from_behind(
                pick_block(shares, target).astype(jnp.bfloat16), "expert", stride * group_width
            ).astype(jnp.float32),
        )
        arrived_rows.append(rows_in)
        arrived_shares.append(shares_in)
    home_order = (own_group - jnp.arange(EXPERTS, dtype=jnp.int32)) % EXPERTS
    rows_by_source = jnp.take(jnp.stack(arrived_rows), home_order, axis=0)
    shares_by_source = jnp.take(jnp.stack(arrived_shares), home_order, axis=0)
    kept_rows, kept_shares = spread(
        rows_by_source[None], shares_by_source[None], own_index, level_values
    )
    slot_rows = kept_rows.reshape(-1, kept_rows.shape[-1])
    slot_shares = kept_shares.reshape(-1)
    gate_part = jnp.dot(slot_rows, w_in[0], preferred_element_type=jnp.float32)
    up_part = jnp.dot(slot_rows, w_in[1], preferred_element_type=jnp.float32)
    hidden = (jax.nn.silu(gate_part) * up_part * slot_shares[:, None]).astype(jnp.bfloat16)
    return (stream_part, hidden)


def solution(mesh):
    placed = (
        P(("groups", "expert"), "sub"),
        P(("groups", "expert"), "sub"),
        P(None, ("groups", "expert"), "sub"),
        P(None, ("groups", "expert"), None, "sub"),
        P(("groups", "expert"), None),
        P(("groups", "expert")),
        P(),
        P(),
        P(("groups", "expert"), None),
        P(None, None, ("expert", "sub")),
    )
    return jax.shard_map(
        shards,
        mesh=mesh,
        in_specs=placed,
        out_specs=(P(("groups", "expert"), "sub"), P("groups", ("expert", "sub"))),
        check_vma=False,
    )
```

profile of v0, /device:TPU:25, one launch (start us, length us, event | category | flops | bytes accessed | tf_op | source)
XLA Modules:
  0.0 103.8 jit_solution(13297511967904677882)
XLA Ops:
  0.7 0.7 fusion.77
  1.5 0.7 copy.83
  2.2 5.5 %all-to-all-start = ((s32[8,1,1]{2,1,0:T(1,128)}), s32[8,1,1]{2,1,0:T(1,128)S(1)}, u32[]{:S(2)}, u32[]{:S(2)}) async-start(s32[8,1,1]{2,1,0:T(1,128)} %copy.83), calls=%async_computation | async-start | bytes 8192 | tf_op jit(solution)/shard_map/all_to_all | solution.py:98
  7.7 0.7 fusion.60
  8.4 0.7 bitcast_or_fusion
  9.0 0.8 copy.90
  11.4 0.7 compare_and_fusion.1
  12.1 1.3 %gather_fusion = bf16[8,2,4,512]{3,2,1,0:T(4,128)(2,1)S(1)} fusion(bf16[2,2,4,512]{3,2,1,0:T(4,128)(2,1)} %param.13, s32[1024]{0:T(1024)S(1)} %pad_clamp_fusion.2), kind=kCustom, calls=%fused_computation | custom fusion | bytes 131104 | tf_op jit(solution)/shard_map/jit(_take)/gather | solution.py:99
  13.4 0.7 select_bitcast_fusion
  14.1 5.4 %all-to-all-start.1 = ((bf16[2,8,4,512]{3,2,0,1:T(4,128)(2,1)}), bf16[2,8,4,512]{3,2,0,1:T(4,128)(2,1)S(1)}, u32[]{:S(2)}, u32[]{:S(2)}) async-start(bf16[2,8,4,512]{3,2,0,1:T(4,128)(2,1)} %select_bitcast_fusion), calls=%async_computation.1 | async-start | bytes 131072 | tf_op jit(solution)/shard_map/all_to_all | solution.py:100
  20.2 2.1 %all-to-all-done.1 = bf16[2,8,4,512]{3,2,0,1:T(4,128)(2,1)S(1)} async-done(((bf16[2,8,4,512]{3,2,0,1:T(4,128)(2,1)}), bf16[2,8,4,512]{3,2,0,1:T(4,128)(2,1)S(1)}, u32[]{:S(2)}, u32[]{:S(2)}) %all-to-all-start.1) | async-done | bytes 65568 | tf_op jit(solution)/shard_map/all_to_all | solution.py:100
  23.9 1.4 %fusion.21 = f32[64,4,3,128]{3,0,2,1:T(8,128)S(1)} fusion(f32[4,3,64]{2,1,0:T(4,128)S(1)} %fusion.81, bf16[96,4,128,1]{2,1,0,3:T(4,128)(2,1)S(1)} %bitcast.148, f32[4,3,64,96]{3,2,1,0:T(8,128)S(1)} %fusion.19), kind=kOutput, calls=%fused_computation.24 | convolution fusion | flops 19293024 | bytes 789504 | tf_op jit(solution)/shard_map/kgtl,lkd->tkgd/dot_general | solution.py:51
  26.4 4.6 %all_gather.3 = bf16[64,3072]{1,0:T(8,128)(2,1)S(1)} all-gather(bf16[64,1536]{1,0:T(8,128)(2,1)S(1)} %add_convert_fusion), channel_id=1, replica_groups=mesh['groups'=2,'expert'=8,'sub'=2] {'sub'}, dimensions={1}, use_global_device_ids=true | all-gather | bytes 589824 | tf_op jit(solution)/shard_map/all_gather | solution.py:108
  31.4 1.0 gather_fusion.4
  33.3 1.0 collective-permute-start.13
  34.3 1.5 %collective-permute-start.12 = (bf16[17]{0:T(256)(128)(2,1)S(1)}, bf16[17]{0:T(256)(128)(2,1)S(1)}, u32[]{:S(2)}, u32[]{:S(2)}) collective-permute-start(bf16[17]{0:T(256)(128)(2,1)S(1)} %get-tuple-element.13), channel_id=1, source_target_pairs={{0,12},{2,14},{4,0},{6,2},{8,4},{10,6},{12,8},{14,10},{1,13},{3,15... | collective-permute-start | bytes 110 | tf_op jit(solution)/shard_map/ppermute | solution.py:29
  35.8 2.0 %collective-permute-start.11 = (bf16[17]{0:T(256)(128)(2,1)S(1)}, bf16[17]{0:T(256)(128)(2,1)S(1)}, u32[]{:S(2)}, u32[]{:S(2)}) collective-permute-start(bf16[17]{0:T(256)(128)(2,1)S(1)} %get-tuple-element.14), channel_id=1, source_target_pairs={{0,10},{2,12},{4,14},{6,0},{8,2},{10,4},{12,6},{14,8},{1,11},{3,13... | collective-permute-start | bytes 110 | tf_op jit(solution)/shard_map/ppermute | solution.py:29
  38.0 2.4 %collective-permute-start.9 = (bf16[17]{0:T(256)(128)(2,1)S(1)}, bf16[17]{0:T(256)(128)(2,1)S(1)}, u32[]{:S(2)}, u32[]{:S(2)}) collective-permute-start(bf16[17]{0:T(256)(128)(2,1)S(1)} %get-tuple-element.16), channel_id=1, source_target_pairs={{0,6},{2,8},{4,10},{6,12},{8,14},{10,0},{12,2},{14,4},{1,7},{3,9},... | collective-permute-start | bytes 110 | tf_op jit(solution)/shard_map/ppermute | solution.py:29
  40.4 0.6 convolution_convert_fusion
  41.1 0.8 collective-permute-start.8
  42.0 1.0 collective-permute-start.7
  43.0 1.4 %collective-permute-start.6 = (bf16[17,3072]{1,0:T(8,128)(2,1)S(1)}, bf16[17,3072]{1,0:T(8,128)(2,1)S(1)}, u32[]{:S(2)}, u32[]{:S(2)}) collective-permute-start(bf16[17,3072]{1,0:T(8,128)(2,1)S(1)} %get-tuple-element.2), channel_id=1, source_target_pairs={{0,14},{2,0},{4,2},{6,4},{8,6},{10,8},{12,10},{14,12},{1,15},{3,1}... | collective-permute-start | bytes 313352 | tf_op jit(solution)/shard_map/ppermute | solution.py:29
  44.3 0.7 collective-permute-start.5
  45.1 2.9 %collective-permute-start.3 = (bf16[17,3072]{1,0:T(8,128)(2,1)S(1)}, bf16[17,3072]{1,0:T(8,128)(2,1)S(1)}, u32[]{:S(2)}, u32[]{:S(2)}) collective-permute-start(bf16[17,3072]{1,0:T(8,128)(2,1)S(1)} %get-tuple-element.5), channel_id=1, source_target_pairs={{0,8},{2,10},{4,12},{6,14},{8,0},{10,2},{12,4},{14,6},{1,9},{3,11}... | collective-permute-start | bytes 313352 | tf_op jit(solution)/shard_map/ppermute | solution.py:29
  48.0 1.2 %collective-permute-start = (bf16[17,3072]{1,0:T(8,128)(2,1)S(1)}, bf16[17,3072]{1,0:T(8,128)(2,1)S(1)}, u32[]{:S(2)}, u32[]{:S(2)}) collective-permute-start(bf16[17,3072]{1,0:T(8,128)(2,1)S(1)} %get-tuple-element.8), channel_id=1, source_target_pairs={{0,2},{2,4},{4,6},{6,8},{8,10},{10,12},{12,14},{14,0},{1,3},{3,5},... | collective-permute-start | bytes 313352 | tf_op jit(solution)/shard_map/ppermute | solution.py:29
  49.9 8.6 %collective-permute-done = bf16[17,3072]{1,0:T(8,128)(2,1)S(1)} collective-permute-done((bf16[17,3072]{1,0:T(8,128)(2,1)S(1)}, bf16[17,3072]{1,0:T(8,128)(2,1)S(1)}, u32[]{:S(2)}, u32[]{:S(2)}) %collective-permute-start) | collective-permute-done | bytes 104480 | tf_op jit(solution)/shard_map/ppermute | solution.py:29
  58.5 1.0 collective-permute-start.1
  59.5 11.4 %collective-permute-done.1 = bf16[17,3072]{1,0:T(8,128)(2,1)S(1)} collective-permute-done((bf16[17,3072]{1,0:T(8,128)(2,1)S(1)}, bf16[17,3072]{1,0:T(8,128)(2,1)S(1)}, u32[]{:S(2)}, u32[]{:S(2)}) %collective-permute-start.1) | collective-permute-done | bytes 104480 | tf_op jit(solution)/shard_map/ppermute | solution.py:29
  70.9 10.3 %collective-permute-done.2 = bf16[17,3072]{1,0:T(8,128)(2,1)S(1)} collective-permute-done((bf16[17,3072]{1,0:T(8,128)(2,1)S(1)}, bf16[17,3072]{1,0:T(8,128)(2,1)S(1)}, u32[]{:S(2)}, u32[]{:S(2)}) %collective-permute-start.2) | collective-permute-done | bytes 104480 | tf_op jit(solution)/shard_map/ppermute | solution.py:29
  81.3 0.6 gather_fusion.2
  82.4 10.1 %fusion.3 = f32[136,4096]{1,0:T(8,128)S(1)} fusion(bf16[136,3072]{1,0:T(8,128)(2,1)S(1)} %select_n.256, bf16[2,3072,4096]{2,1,0:T(8,128)(2,1)} %param.19), kind=kOutput, calls=%fused_computation.8 | convolution fusion | flops 3422552064 | bytes 28229632 | tf_op jit(solution)/shard_map/dot_general | solution.py:154
  92.5 11.3 %fusion.13 = bf16[136,4096]{1,0:T(8,128)(2,1)} fusion(bf16[136,3072]{1,0:T(8,128)(2,1)S(1)} %select_n.256, bf16[2,3072,4096]{2,1,0:T(8,128)(2,1)} %param.19, f32[136,4096]{1,0:T(8,128)S(1)} %fusion.3, f32[136]{0:T(256)S(1)} %select_n.260), kind=kOutput, calls=%fused_computation.14 | convolution fusion | flops 3426451456 | bytes 29344288 | tf_op jit(solution)/shard_map/dot_general | solution.py:155
  (99 shorter events, 7.0 us)
Async XLA Ops:
  0.6 30.5 %copy-start = (bf16[3072,8]{0,1:T(8,128)(2,1)S(1)}, bf16[3072,8]{0,1:T(8,128)(2,1)}, u32[]{:S(2)}) copy-start(bf16[3072,8]{0,1:T(8,128)(2,1)} %param.17) | copy-start | bytes 147460
  0.6 19.2 %copy-start.2 = (bf16[64,1536]{1,0:T(8,128)(2,1)S(1)}, bf16[64,1536]{1,0:T(8,128)(2,1)}, u32[]{:S(2)}) copy-start(bf16[64,1536]{1,0:T(8,128)(2,1)} %param.11) | copy-start | bytes 589828
  0.7 22.5 %copy-start.4 = (bf16[2,64,512]{2,1,0:T(8,128)(2,1)S(1)}, bf16[2,64,512]{2,1,0:T(8,128)(2,1)}, u32[]{:S(2)}) copy-start(bf16[2,64,512]{2,1,0:T(8,128)(2,1)} %param.12) | copy-start | bytes 393220
  2.2 8.9 %all-to-all-start = ((s32[8,1,1]{2,1,0:T(1,128)}), s32[8,1,1]{2,1,0:T(1,128)S(1)}, u32[]{:S(2)}, u32[]{:S(2)}) async-start(s32[8,1,1]{2,1,0:T(1,128)} %copy.83), calls=%async_computation | async-start | bytes 8192 | tf_op jit(solution)/shard_map/all_to_all | solution.py:98
  14.1 8.2 %all-to-all-start.1 = ((bf16[2,8,4,512]{3,2,0,1:T(4,128)(2,1)}), bf16[2,8,4,512]{3,2,0,1:T(4,128)(2,1)S(1)}, u32[]{:S(2)}, u32[]{:S(2)}) async-start(bf16[2,8,4,512]{3,2,0,1:T(4,128)(2,1)} %select_bitcast_fusion), calls=%async_computation.1 | async-start | bytes 131072 | tf_op jit(solution)/shard_map/all_to_all | solution.py:100
  25.4 0.9 copy-start.3
  25.6 5.5 %copy-start.5 = (f32[3072]{0:T(1024)S(1)}, f32[3072]{0:T(1024)}, u32[]{:S(2)}) copy-start(f32[3072]{0:T(1024)} %param.16) | copy-start | bytes 36868
  26.3 6.1 %copy-start.1 = (bf16[64,1536]{1,0:T(8,128)(2,1)}, bf16[64,1536]{1,0:T(8,128)(2,1)S(1)}, u32[]{:S(2)}) copy-start(bf16[64,1536]{1,0:T(8,128)(2,1)S(1)} %add_convert_fusion) | copy-start | bytes 589828
  31.4 1.3 %copy-start.6 = (s32[64,2]{0,1:T(2,128)S(1)}, s32[64,2]{0,1:T(2,128)}, u32[]{:S(2)}) copy-start(s32[64,2]{0,1:T(2,128)} %param.18) | copy-start | bytes 1540
  33.3 7.8 %collective-permute-start.13 = (bf16[17]{0:T(256)(128)(2,1)S(1)}, bf16[17]{0:T(256)(128)(2,1)S(1)}, u32[]{:S(2)}, u32[]{:S(2)}) collective-permute-start(bf16[17]{0:T(256)(128)(2,1)S(1)} %get-tuple-element.12), channel_id=1, source_target_pairs={{0,14},{2,0},{4,2},{6,4},{8,6},{10,8},{12,10},{14,12},{1,15},{3,1}... | collective-permute-start | bytes 110 | tf_op jit(solution)/shard_map/ppermute | solution.py:29
  34.3 7.7 %collective-permute-start.12 = (bf16[17]{0:T(256)(128)(2,1)S(1)}, bf16[17]{0:T(256)(128)(2,1)S(1)}, u32[]{:S(2)}, u32[]{:S(2)}) collective-permute-start(bf16[17]{0:T(256)(128)(2,1)S(1)} %get-tuple-element.13), channel_id=1, source_target_pairs={{0,12},{2,14},{4,0},{6,2},{8,4},{10,6},{12,8},{14,10},{1,13},{3,15... | collective-permute-start | bytes 110 | tf_op jit(solution)/shard_map/ppermute | solution.py:29
  35.8 7.2 %collective-permute-start.11 = (bf16[17]{0:T(256)(128)(2,1)S(1)}, bf16[17]{0:T(256)(128)(2,1)S(1)}, u32[]{:S(2)}, u32[]{:S(2)}) collective-permute-start(bf16[17]{0:T(256)(128)(2,1)S(1)} %get-tuple-element.14), channel_id=1, source_target_pairs={{0,10},{2,12},{4,14},{6,0},{8,2},{10,4},{12,6},{14,8},{1,11},{3,13... | collective-permute-start | bytes 110 | tf_op jit(solution)/shard_map/ppermute | solution.py:29
  37.8 6.6 %collective-permute-start.10 = (bf16[17]{0:T(256)(128)(2,1)S(1)}, bf16[17]{0:T(256)(128)(2,1)S(1)}, u32[]{:S(2)}, u32[]{:S(2)}) collective-permute-start(bf16[17]{0:T(256)(128)(2,1)S(1)} %get-tuple-element.15), channel_id=1, source_target_pairs={{0,8},{2,10},{4,12},{6,14},{8,0},{10,2},{12,4},{14,6},{1,9},{3,11}... | collective-permute-start | bytes 110 | tf_op jit(solution)/shard_map/ppermute | solution.py:29
  38.0 7.0 %collective-permute-start.9 = (bf16[17]{0:T(256)(128)(2,1)S(1)}, bf16[17]{0:T(256)(128)(2,1)S(1)}, u32[]{:S(2)}, u32[]{:S(2)}) collective-permute-start(bf16[17]{0:T(256)(128)(2,1)S(1)} %get-tuple-element.16), channel_id=1, source_target_pairs={{0,6},{2,8},{4,10},{6,12},{8,14},{10,0},{12,2},{14,4},{1,7},{3,9},... | collective-permute-start | bytes 110 | tf_op jit(solution)/shard_map/ppermute | solution.py:29
  41.1 3.9 %collective-permute-start.8 = (bf16[17]{0:T(256)(128)(2,1)S(1)}, bf16[17]{0:T(256)(128)(2,1)S(1)}, u32[]{:S(2)}, u32[]{:S(2)}) collective-permute-start(bf16[17]{0:T(256)(128)(2,1)S(1)} %get-tuple-element.17), channel_id=1, source_target_pairs={{0,4},{2,6},{4,8},{6,10},{8,12},{10,14},{12,0},{14,2},{1,5},{3,7},... | collective-permute-start | bytes 110 | tf_op jit(solution)/shard_map/ppermute | solution.py:29
  42.0 6.0 %collective-permute-start.7 = (bf16[17]{0:T(256)(128)(2,1)S(1)}, bf16[17]{0:T(256)(128)(2,1)S(1)}, u32[]{:S(2)}, u32[]{:S(2)}) collective-permute-start(bf16[17]{0:T(256)(128)(2,1)S(1)} %get-tuple-element.18), channel_id=1, source_target_pairs={{0,2},{2,4},{4,6},{6,8},{8,10},{10,12},{12,14},{14,0},{1,3},{3,5},... | collective-permute-start | bytes 110 | tf_op jit(solution)/shard_map/ppermute | solution.py:29
  43.0 38.3 %collective-permute-start.6 = (bf16[17,3072]{1,0:T(8,128)(2,1)S(1)}, bf16[17,3072]{1,0:T(8,128)(2,1)S(1)}, u32[]{:S(2)}, u32[]{:S(2)}) collective-permute-start(bf16[17,3072]{1,0:T(8,128)(2,1)S(1)} %get-tuple-element.2), channel_id=1, source_target_pairs={{0,14},{2,0},{4,2},{6,4},{8,6},{10,8},{12,10},{14,12},{1,15},{3,1}... | collective-permute-start | bytes 313352 | tf_op jit(solution)/shard_map/ppermute | solution.py:29
  44.3 36.9 %collective-permute-start.5 = (bf16[17,3072]{1,0:T(8,128)(2,1)S(1)}, bf16[17,3072]{1,0:T(8,128)(2,1)S(1)}, u32[]{:S(2)}, u32[]{:S(2)}) collective-permute-start(bf16[17,3072]{1,0:T(8,128)(2,1)S(1)} %get-tuple-element.3), channel_id=1, source_target_pairs={{0,12},{2,14},{4,0},{6,2},{8,4},{10,6},{12,8},{14,10},{1,13},{3,15... | collective-permute-start | bytes 313352 | tf_op jit(solution)/shard_map/ppermute | solution.py:29
  45.0 36.2 %collective-permute-start.4 = (bf16[17,3072]{1,0:T(8,128)(2,1)S(1)}, bf16[17,3072]{1,0:T(8,128)(2,1)S(1)}, u32[]{:S(2)}, u32[]{:S(2)}) collective-permute-start(bf16[17,3072]{1,0:T(8,128)(2,1)S(1)} %get-tuple-element.4), channel_id=1, source_target_pairs={{0,10},{2,12},{4,14},{6,0},{8,2},{10,4},{12,6},{14,8},{1,11},{3,13... | collective-permute-start | bytes 313352 | tf_op jit(solution)/shard_map/ppermute | solution.py:29
  45.1 36.1 %collective-permute-start.3 = (bf16[17,3072]{1,0:T(8,128)(2,1)S(1)}, bf16[17,3072]{1,0:T(8,128)(2,1)S(1)}, u32[]{:S(2)}, u32[]{:S(2)}) collective-permute-start(bf16[17,3072]{1,0:T(8,128)(2,1)S(1)} %get-tuple-element.5), channel_id=1, source_target_pairs={{0,8},{2,10},{4,12},{6,14},{8,0},{10,2},{12,4},{14,6},{1,9},{3,11}... | collective-permute-start | bytes 313352 | tf_op jit(solution)/shard_map/ppermute | solution.py:29
  48.0 10.5 %collective-permute-start = (bf16[17,3072]{1,0:T(8,128)(2,1)S(1)}, bf16[17,3072]{1,0:T(8,128)(2,1)S(1)}, u32[]{:S(2)}, u32[]{:S(2)}) collective-permute-start(bf16[17,3072]{1,0:T(8,128)(2,1)S(1)} %get-tuple-element.8), channel_id=1, source_target_pairs={{0,2},{2,4},{4,6},{6,8},{8,10},{10,12},{12,14},{14,0},{1,3},{3,5},... | collective-permute-start | bytes 313352 | tf_op jit(solution)/shard_map/ppermute | solution.py:29
  58.5 12.4 %collective-permute-start.1 = (bf16[17,3072]{1,0:T(8,128)(2,1)S(1)}, bf16[17,3072]{1,0:T(8,128)(2,1)S(1)}, u32[]{:S(2)}, u32[]{:S(2)}) collective-permute-start(bf16[17,3072]{1,0:T(8,128)(2,1)S(1)} %get-tuple-element.7), channel_id=1, source_target_pairs={{0,4},{2,6},{4,8},{6,10},{8,12},{10,14},{12,0},{14,2},{1,5},{3,7},... | collective-permute-start | bytes 313352 | tf_op jit(solution)/shard_map/ppermute | solution.py:29
  70.9 10.3 %collective-permute-start.2 = (bf16[17,3072]{1,0:T(8,128)(2,1)S(1)}, bf16[17,3072]{1,0:T(8,128)(2,1)S(1)}, u32[]{:S(2)}, u32[]{:S(2)}) collective-permute-start(bf16[17,3072]{1,0:T(8,128)(2,1)S(1)} %get-tuple-element.6), channel_id=1, source_target_pairs={{0,6},{2,8},{4,10},{6,12},{8,14},{10,0},{12,2},{14,4},{1,7},{3,9},... | collective-permute-start | bytes 313352 | tf_op jit(solution)/shard_map/ppermute | solution.py:29
where the time goes:
time: 104 us
  waiting for transfers between devices  32.4 us (31%)
  starting transfers between devices  26.9 us (26%)
  matrix products  24.5 us (24%)
  local copies, waits for them, and re-layouts  8.52 us (8%)
  other arithmetic  5 us (5%)
  blocking collectives  4.6 us (4%)
  between operations  1.78 us (2%)
    ppermute x14, waiting for transfers between devices, from_behind(): return lax.ppermute(value, axis, pairs)  30.3 us
    ppermute x14, starting transfers between devices, from_behind(): return lax.ppermute(value, axis, pairs)  16 us
    dot_general x1, matrix products, shards(): up_part = jnp.dot(slot_rows, w_in[1], preferred_element_type=jnp.float32)  11.3 us
    dot_general x1, matrix products, shards(): gate_part = jnp.dot(slot_rows, w_in[0], preferred_element_type=jnp.float32)  10.1 us
    all_to_all x1, starting transfers between devices, shards(): lax.all_to_all(wanted[:, None], 'expert', split_axis=0, concat_axis=0, ti...  5.47 us
    all_to_all x1, starting transfers between devices, shards(): lax.all_to_all(served, 'expert', split_axis=1, concat_axis=1, tiled=True)  5.44 us
    all_gather x1, blocking collectives, shards(): stream = lax.all_gather(stream_part, 'sub', axis=1, tiled=True)  4.6 us
    all_to_all x1, waiting for transfers between devices, shards(): lax.all_to_all(served, 'expert', split_axis=1, concat_axis=1, tiled=True)  2.11 us
  transfers between devices with their start and end apart: 16, of which 4 were waited for; matrix products, arithmetic and copies ran while one was open for 5% of the time, Pallas kernels for 0%

commit v1 on v0

v1 whole, which is shorter than its diff:
```python
import math

import jax
import jax.numpy as jnp
from jax import lax
from jax.experimental import pallas as pl
from jax.experimental.pallas import tpu as pltpu
from jax.sharding import PartitionSpec as P

HEAD_WIDTH = 128
EXPERTS = 8
CAP = 17
MAIN = 16
LANES = 128
F32 = jnp.float32
BF16 = jnp.bfloat16
MESH = pl.DeviceIdType.MESH


def dot(a, b):
    return jnp.dot(a, b, preferred_element_type=F32)


def iota(shape, dim):
    return lax.broadcasted_iota(jnp.int32, shape, dim)


def kernel(
    count,
    w_chunks,
    page_tokens,
    page_table,
    prefix_len,
    stream_in,
    queries,
    kv_new,
    cache,
    norm_gain,
    w_router,
    expert_ids,
    w_in,
    stream_out,
    hidden_out,
    weights,
    kv_all,
    part,
    part_in,
    rows_out,
    last_out,
    rows_in,
    last_in,
    rows_over,
    last_over,
    slots,
    w_sem,
    page_send,
    page_recv,
    part_send,
    part_recv,
    row_send,
    row_recv,
    last_send,
    last_recv,
    over_send,
    over_recv,
    over_last_send,
    over_last_recv,
):
    me = lax.axis_index("expert")
    core = lax.axis_index("sub")
    width = count // EXPERTS
    half = stream_in.shape[1]
    tokens = stream_in.shape[0]
    holder = me // width

    def place(index):
        return (index % width) * EXPERTS + index // width

    barrier = pltpu.get_barrier_semaphore()

    def greet(step, carry):
        pl.semaphore_signal(
            barrier, inc=1, device_id={"expert": (me + step) % count}, device_id_type=MESH
        )
        return carry

    lax.fori_loop(1, count, greet, 0)
    pl.semaphore_signal(barrier, inc=1, device_id={"sub": 1 - core}, device_id_type=MESH)

    depth = weights.shape[1] // w_chunks
    loads = []
    for chunk in range(w_chunks):
        for side in range(2):
            span = pl.ds(chunk * depth, depth)
            load = pltpu.make_async_copy(
                w_in.at[side, span], weights.at[side, span], w_sem.at[side, chunk]
            )
            load.start()
            loads.append(load)

    pl.semaphore_wait(barrier, count)

    def page_copy(step):
        return pltpu.make_async_remote_copy(
            src_ref=cache,
            dst_ref=kv_all.at[me],
            send_sem=page_send.at[step],
            recv_sem=page_recv.at[step],
            device_id={"expert": (me + step) % count},
            device_id_type=MESH,
        )

    def start_pages(step, carry):
        page_copy(step).start()
        return carry

    lax.fori_loop(1, count, start_pages, 0)
    kv_all[me] = cache[...]

    shard_rows = cache.shape[1]
    page_rows = kv_all.shape[0] * shard_rows
    table_pages = page_table.shape[1]
    tokens_page = page_tokens
    key_heads = kv_new.shape[2] // HEAD_WIDTH
    grouped = half // HEAD_WIDTH // key_heads
    scaling = 1.0 / math.sqrt(HEAD_WIDTH)
    flat = ((1,), (1,)), ((), ())
    stacked = tokens * grouped
    causal = iota((stacked, tokens), 1) <= iota((stacked, tokens), 0) % tokens
    asked = []
    own_scores = []
    for head in range(key_heads):
        lanes = slice(head * HEAD_WIDTH, (head + 1) * HEAD_WIDTH)
        query = jnp.concatenate(
            [
                queries[:, (head * grouped + g) * HEAD_WIDTH : (head * grouped + g + 1) * HEAD_WIDTH]
                for g in range(grouped)
            ],
            axis=0,
        )
        asked.append(query)
        score = lax.dot_general(query, kv_new[0, :, lanes], flat, preferred_element_type=F32)
        own_scores.append(jnp.where(causal, score * scaling, -1e30))

    row_at = iota((1, page_rows), 1)
    page_at = row_at // tokens_page

    def find(j, found):
        return jnp.where(page_at == page_table[0, j], j * tokens_page, found)

    never = jnp.full((1, page_rows), 1 << 29, jnp.int32)
    position = lax.fori_loop(0, table_pages, find, never) + row_at % tokens_page
    alive = position < prefix_len[0]

    def wait_pages(step, carry):
        page_copy(step).wait()
        return carry

    lax.fori_loop(1, count, wait_pages, 0)

    for head in range(key_heads):
        lanes = slice(head * HEAD_WIDTH, (head + 1) * HEAD_WIDTH)
        keys = kv_all[:, 0, :, lanes].astype(F32).reshape(page_rows, HEAD_WIDTH).astype(BF16)
        values = kv_all[:, 1, :, lanes].astype(F32).reshape(page_rows, HEAD_WIDTH).astype(BF16)
        old = lax.dot_general(asked[head], keys, flat, preferred_element_type=F32) * scaling
        old = jnp.where(alive, old, -1e30)
        new = own_scores[head]
        largest = jnp.maximum(
            jnp.max(old, axis=1, keepdims=True), jnp.max(new, axis=1, keepdims=True)
        )
        old = jnp.exp(old - largest)
        new = jnp.exp(new - largest)
        total = jnp.sum(old, axis=1, keepdims=True) + jnp.sum(new, axis=1, keepdims=True)
        mixed = dot((old / total).astype(BF16), values)
        mixed = mixed + dot((new / total).astype(BF16), kv_new[1, :, lanes])
        mixed = mixed.astype(BF16).astype(F32)
        for g in range(grouped):
            at = slice((head * grouped + g) * HEAD_WIDTH, (head * grouped + g + 1) * HEAD_WIDTH)
            stream_out[:, at] = (
                stream_in[:, at].astype(F32) + mixed[g * tokens : (g + 1) * tokens]
            ).astype(BF16)

    stream = stream_out[...].astype(F32)
    first = pl.multiple_of(core * half, LANES)
    gain = norm_gain[:, pl.ds(first, half)]
    squares = jnp.sum(stream * stream, axis=1, keepdims=True)
    raw = dot((stream * gain).astype(BF16), w_router[pl.ds(first, half), :])
    part[0] = jnp.zeros((tokens, LANES), F32)
    part[0, :, 0:EXPERTS] = raw
    part[1] = jnp.broadcast_to(squares, (tokens, LANES))
    swap = pltpu.make_async_remote_copy(
        src_ref=part,
        dst_ref=part_in,
        send_sem=part_send,
        recv_sem=part_recv,
        device_id={"sub": 1 - core},
        device_id_type=MESH,
    )
    swap.start()

    lane = iota((tokens, LANES), 1)
    named = (expert_ids[:, 0:1] == lane) | (expert_ids[:, 1:2] == lane)
    hot = named.astype(F32)
    hot_b = hot.astype(BF16)
    before = (iota((tokens, tokens), 0) < iota((tokens, tokens), 1)).astype(F32).astype(BF16)
    same = (iota((tokens, tokens), 0) == iota((tokens, tokens), 1)).astype(F32).astype(BF16)
    turn = ((0,), (0,)), ((), ())
    rank = lax.dot_general(hot_b, before, turn, preferred_element_type=F32)[0:EXPERTS]
    is_hot = lax.dot_general(hot_b, same, turn, preferred_element_type=F32)[0:EXPERTS]
    rank = jnp.where(is_hot > 0.5, rank, -1.0)
    slot = iota((MAIN, tokens), 0).astype(F32)
    picker = jnp.concatenate(
        [
            (jnp.broadcast_to(rank[e : e + 1], (MAIN, tokens)) == slot).astype(F32)
            for e in range(EXPERTS)
        ],
        axis=0,
    ).astype(BF16)
    last_picker = (rank == float(MAIN)).astype(F32).astype(BF16)

    swap.wait()
    scale = lax.rsqrt((part[1] + part_in[1])[:, 0:1] / (2 * half) + 1e-05)
    logits = (part[0] + part_in[0]) * scale
    chosen = logits * hot
    both = jnp.sum(chosen, axis=1, keepdims=True)
    share = jnp.where(named, 1.0 / (1.0 + jnp.exp(both - 2.0 * chosen)), 0.0)
    high = share.astype(BF16).astype(F32)
    shares = (high + pltpu.roll(share - high, EXPERTS, 1)).astype(BF16)
    normed = (stream * scale * gain).astype(BF16)
    normed = jnp.concatenate([normed, shares], axis=1)
    picked = dot(picker, normed).astype(BF16)
    last = dot(last_picker, normed)
    for e in range(EXPERTS):
        rows_out[e] = picked[e * MAIN : (e + 1) * MAIN]
        last_out[e] = last[e : e + 1]

    def row_copies(step):
        to = (me + step) % count
        mine = place(me)
        return (
            pltpu.make_async_remote_copy(
                src_ref=rows_out.at[to // width],
                dst_ref=rows_in.at[mine],
                send_sem=row_send.at[step],
                recv_sem=row_recv.at[step],
                device_id={"expert": to},
                device_id_type=MESH,
            ),
            pltpu.make_async_remote_copy(
                src_ref=last_out.at[to // width],
                dst_ref=last_in.at[mine],
                send_sem=last_send.at[step],
                recv_sem=last_recv.at[step],
                device_id={"expert": to},
                device_id_type=MESH,
            ),
        )

    def over_copies(step):
        at = place((me - step + count) % count)
        return (
            pltpu.make_async_remote_copy(
                src_ref=rows_in.at[at, :, pl.ds(0, half)],
                dst_ref=rows_over.at[at],
                send_sem=over_send.at[step],
                recv_sem=over_recv.at[step],
                device_id={"sub": 1 - core},
                device_id_type=MESH,
            ),
            pltpu.make_async_remote_copy(
                src_ref=last_in.at[at, :, pl.ds(0, half)],
                dst_ref=last_over.at[at],
                send_sem=over_last_send.at[step],
                recv_sem=over_last_recv.at[step],
                device_id={"sub": 1 - core},
                device_id_type=MESH,
            ),
        )

    def start_rows(step, carry):
        for copy in row_copies(step):
            copy.start()
        return carry

    lax.fori_loop(1, count, start_rows, 0)
    rows_in[place(me)] = rows_out[holder]
    last_in[place(me)] = last_out[holder]
    for copy in over_copies(0):
        copy.start()

    def hand_on(step, carry):
        for copy in row_copies(step):
            copy.wait()
        for copy in over_copies(step):
            copy.start()
        return carry

    lax.fori_loop(1, count, hand_on, 0)

    span = EXPERTS * MAIN
    rows = EXPERTS * CAP
    wide = span + MAIN
    to_row = iota((rows, wide), 0)
    from_row = iota((rows, wide), 1)
    source = jnp.where(
        from_row < span, from_row + from_row // MAIN, (from_row - span) * CAP + MAIN
    )
    order = (to_row == source).astype(F32).astype(BF16)

    def lined_up(block, rows_ref, last_ref, lanes):
        at = pl.ds(block * EXPERTS, EXPERTS)
        main = rows_ref[at, :, lanes].reshape(span, -1)
        ends = [last_ref[block * EXPERTS + q, :, lanes] for q in range(EXPERTS)]
        ends.append(jnp.zeros((MAIN - EXPERTS, main.shape[1]), F32))
        tail = jnp.concatenate(ends, axis=0).astype(BF16)
        return dot(order, jnp.concatenate([main, tail], axis=0))

    def own_half(block, carry):
        slots[core, block] = lined_up(block, rows_in, last_in, slice(0, half)).astype(BF16)
        return carry

    lax.fori_loop(0, width, own_half, 0)

    def wait_over(step, carry):
        for copy in over_copies(step):
            copy.wait()
        return carry

    lax.fori_loop(0, count, wait_over, 0)

    def other_half(block, carry):
        slots[1 - core, block] = lined_up(block, rows_over, last_over, slice(0, half)).astype(BF16)
        return carry

    lax.fori_loop(0, width, other_half, 0)
    for load in loads:
        load.wait()

    columns = weights.shape[2]
    tile = min(256, columns)

    def block_rows(block, carry):
        share_rows = lined_up(block, rows_in, last_in, slice(half, half + LANES))
        share_lane = iota((rows, LANES), 1)
        wanted = (share_lane == holder) | (share_lane == holder + EXPERTS)
        slot_share = jnp.sum(jnp.where(wanted, share_rows, 0.0), axis=1, keepdims=True)

        def one_tile(index, inner):
            at = pl.ds(pl.multiple_of(index * tile, tile), tile)

            def product(side):
                return dot(slots[0, block], weights[side, 0:half, at]) + dot(
                    slots[1, block], weights[side, half : 2 * half, at]
                )

            gate = product(0)
            up = product(1)
            hidden_out[block, :, at] = (gate / (1.0 + jnp.exp(-gate)) * up * slot_share).astype(
                BF16
            )
            return inner

        lax.fori_loop(0, columns // tile, one_tile, 0)
        return carry

    lax.fori_loop(0, width, block_rows, 0)


def shards(
    stream_in,
    queries,
    kv_new,
    paged_key_value_cache,
    page_table,
    prefix_len,
    norm_gain,
    w_router,
    expert_ids,
    w_in,
):
    count = lax.axis_size("expert")
    width = count // EXPERTS
    tokens, half = stream_in.shape
    columns = w_in.shape[2]
    cache = paged_key_value_cache.reshape(2, -1, paged_key_value_cache.shape[-1])
    w_chunks = 6
    rows = EXPERTS * CAP
    vmem = pl.BlockSpec(memory_space=pltpu.VMEM)
    smem = pl.BlockSpec(memory_space=pltpu.SMEM)
    dma = pltpu.SemaphoreType.DMA
    stream, hidden = pl.pallas_call(
        lambda *refs: kernel(count, w_chunks, paged_key_value_cache.shape[2], *refs),
        name="moe_prefill",
        out_shape=(
            jax.ShapeDtypeStruct((tokens, half), BF16),
            jax.ShapeDtypeStruct((width, rows, columns), BF16),
        ),
        in_specs=[smem, smem] + [vmem] * 7 + [pl.BlockSpec(memory_space=pl.ANY)],
        out_specs=(vmem, vmem),
        scratch_shapes=[
            pltpu.VMEM(w_in.shape, BF16),
            pltpu.VMEM((count,) + cache.shape, BF16),
            pltpu.VMEM((2, tokens, LANES), F32),
            pltpu.VMEM((2, tokens, LANES), F32),
            pltpu.VMEM((EXPERTS, MAIN, half + LANES), BF16),
            pltpu.VMEM((EXPERTS, 1, half + LANES), F32),
            pltpu.VMEM((count, MAIN, half + LANES), BF16),
            pltpu.VMEM((count, 1, half + LANES), F32),
            pltpu.VMEM((count, MAIN, half), BF16),
            pltpu.VMEM((count, 1, half), F32),
            pltpu.VMEM((2, width, rows, half), BF16),
            dma((2, w_chunks)),
            dma((count,)),
            dma((count,)),
            dma,
            dma,
        ]
        + [dma((count,))] * 8,
        compiler_params=pltpu.CompilerParams(
            collective_id=0, has_side_effects=True, vmem_limit_bytes=67043328
        ),
    )(
        page_table,
        prefix_len,
        stream_in,
        queries,
        kv_new,
        cache,
        norm_gain.reshape(1, -1),
        w_router,
        expert_ids,
        w_in,
    )
    return stream, hidden.reshape(width * rows, columns)


def solution(mesh):
    placed = (
        P(("groups", "expert"), "sub"),
        P(("groups", "expert"), "sub"),
        P(None, ("groups", "expert"), "sub"),
        P(None, ("groups", "expert"), None, "sub"),
        P(("groups", "expert"), None),
        P(("groups", "expert")),
        P(),
        P(),
        P(("groups", "expert"), None),
        P(None, None, ("expert", "sub")),
    )
    return jax.shard_map(
        shards,
        mesh=mesh,
        in_specs=placed,
        out_specs=(P(("groups", "expert"), "sub"), P("groups", ("expert", "sub"))),
        check_vma=False,
    )
```

time: 104 us -> 49.1 us (0.47)
  the two profiles are of different devices: /device:TPU:25 before, /device:TPU:13 now
where the time goes in v1:
time: 49.1 us; the launch traced here: 48.8 us
  Pallas kernels  38.9 us (79%)
  local copies, waits for them, and re-layouts  8.61 us (18%)
  between operations  1.29 us (3%)
    pallas_call x1, Pallas kernels, shards(): pl.pallas_call(lambda *refs: kernel(count, w_chunks, paged_key_value_cach...  38.9 us
    unnamed x4, local copies, waits for them, and re-layouts  7.29 us
    reshape x1, local copies, waits for them, and re-layouts, shards(): paged_key_value_cache.reshape(2, -1, paged_key_value_cache.shape[-1])  1.33 us

profile of v1, /device:TPU:13, one launch (start us, length us, event | category | flops | bytes accessed | tf_op | source)
XLA Modules:
  0.0 48.8 jit_solution(701738728631660463)
XLA Ops:
  1.3 1.3 %reshape.13.refs_5_ = bf16[2,8,512]{2,1,0:T(8,128)(2,1)} reshape(bf16[2,2,4,512]{3,2,1,0:T(4,128)(2,1)} %param.13) | data formatting | bytes 32768 | tf_op jit(solution)/shard_map/reshape | solution.py:385
  2.6 1.4 %copy.13.refs_8_ = s32[64,2]{1,0:T(8,128)} copy(s32[64,2]{0,1:T(2,128)} %param.18) | data formatting | bytes 1024 | tf_op args[8]
  4.0 2.0 %copy.12.refs_7_ = bf16[3072,8]{1,0:T(8,128)(2,1)} copy(bf16[3072,8]{0,1:T(8,128)(2,1)} %param.17) | data formatting | bytes 98304 | tf_op args[7]
  5.9 38.9 %moe_prefill.1 = (bf16[64,1536]{1,0:T(8,128)(2,1)}, bf16[1,136,4096]{2,1,0:T(8,128)(2,1)}) custom-call(s32[1,8]{1,0:T(1,128)} %refs_0_.1, s32[1]{0:T(128)S(6)} %copy.16.refs_1_, bf16[64,1536]{1,0:T(8,128)(2,1)} %refs_2_.1, bf16[64,1536]{1,0:T(8,128)(2,1)} %refs_3_.1, bf16[2,64,512]{2,1,0:T(8,128)(2,1)} %refs_4_.1, bf16[2,8,512]{2,1,0:T(8,128)(2,1)} %reshape.13.refs_5_, ...), custom_call_target="tpu_custom_call" | custom-call | tf_op jit(solution)/shard_map/moe_prefill/pallas_call | solution.py:391
  44.8 1.6 %copy.17 = bf16[64,1536]{1,0:T(8,128)(2,1)} copy(bf16[64,1536]{1,0:T(8,128)(2,1)} %get-tuple-element.8) | data formatting | bytes 393216
  46.4 2.3 %copy.18 = bf16[136,4096]{1,0:T(8,128)(2,1)} copy(bf16[136,4096]{1,0:T(8,128)(2,1)} %bitcast.2) | data formatting | bytes 2228224

commit v2 on v1

--- a/solution.py
+++ b/solution.py
@@ -31,16 +31,28 @@
     page_tokens,
     page_table,
     prefix_len,
-    stream_in,
+    cache_hbm,
+    queries_hbm,
+    kv_new_hbm,
+    stream_hbm,
+    norm_gain_hbm,
+    w_router_hbm,
+    expert_ids_hbm,
+    w_in,
+    stream_result,
+    hidden_result,
+    cache,
     queries,
     kv_new,
-    cache,
+    stream_in,
     norm_gain,
     w_router,
     expert_ids,
-    w_in,
     stream_out,
     hidden_out,
+    in_sem,
+    stream_sem,
+    hidden_sem,
     weights,
     kv_all,
     part,
@@ -76,6 +88,21 @@
     def place(index):
         return (index % width) * EXPERTS + index // width
 
+    pairs = (
+        (cache_hbm, cache),
+        (queries_hbm, queries),
+        (kv_new_hbm, kv_new),
+        (stream_hbm, stream_in),
+        (norm_gain_hbm, norm_gain),
+        (w_router_hbm, w_router),
+        (expert_ids_hbm, expert_ids),
+    )
+    taken = [
+        pltpu.make_async_copy(far, near, in_sem.at[index])
+        for index, (far, near) in enumerate(pairs)
+    ]
+    for copy in taken:
+        copy.start()
     barrier = pltpu.get_barrier_semaphore()
 
     def greet(step, carry):
@@ -98,6 +125,7 @@
             load.start()
             loads.append(load)
 
+    taken[0].wait()
     pl.semaphore_wait(barrier, count)
 
     def page_copy(step):
@@ -116,8 +144,11 @@
 
     lax.fori_loop(1, count, start_pages, 0)
     kv_all[me] = cache[...]
-
-    shard_rows = cache.shape[1]
+    for copy in taken[1:]:
+        copy.wait()
+
+    shard_pages = cache.shape[1]
+    shard_rows = shard_pages * page_tokens
     page_rows = kv_all.shape[0] * shard_rows
     table_pages = page_table.shape[1]
     tokens_page = page_tokens
@@ -152,6 +183,11 @@
     position = lax.fori_loop(0, table_pages, find, never) + row_at % tokens_page
     alive = position < prefix_len[0]
 
+    def cached(kind, lanes):
+        pages = [kv_all[:, kind, p, :, lanes].astype(F32) for p in range(shard_pages)]
+        joined = jnp.concatenate(pages, axis=1)
+        return joined.reshape(page_rows, HEAD_WIDTH).astype(BF16)
+
     def wait_pages(step, carry):
         page_copy(step).wait()
         return carry
@@ -160,8 +196,8 @@
 
     for head in range(key_heads):
         lanes = slice(head * HEAD_WIDTH, (head + 1) * HEAD_WIDTH)
-        keys = kv_all[:, 0, :, lanes].astype(F32).reshape(page_rows, HEAD_WIDTH).astype(BF16)
-        values = kv_all[:, 1, :, lanes].astype(F32).reshape(page_rows, HEAD_WIDTH).astype(BF16)
+        keys = cached(0, lanes)
+        values = cached(1, lanes)
         old = lax.dot_general(asked[head], keys, flat, preferred_element_type=F32) * scaling
         old = jnp.where(alive, old, -1e30)
         new = own_scores[head]
@@ -180,11 +216,18 @@
                 stream_in[:, at].astype(F32) + mixed[g * tokens : (g + 1) * tokens]
             ).astype(BF16)
 
+    keep = pltpu.make_async_copy(stream_out, stream_result, stream_sem)
+    keep.start()
     stream = stream_out[...].astype(F32)
     first = pl.multiple_of(core * half, LANES)
     gain = norm_gain[:, pl.ds(first, half)]
     squares = jnp.sum(stream * stream, axis=1, keepdims=True)
-    raw = dot((stream * gain).astype(BF16), w_router[pl.ds(first, half), :])
+    raw = lax.dot_general(
+        (stream * gain).astype(BF16),
+        w_router[:, pl.ds(first, half)],
+        flat,
+        preferred_element_type=F32,
+    )
     part[0] = jnp.zeros((tokens, LANES), F32)
     part[0, :, 0:EXPERTS] = raw
     part[1] = jnp.broadcast_to(squares, (tokens, LANES))
@@ -198,16 +241,14 @@
     )
     swap.start()
 
-    lane = iota((tokens, LANES), 1)
-    named = (expert_ids[:, 0:1] == lane) | (expert_ids[:, 1:2] == lane)
-    hot = named.astype(F32)
-    hot_b = hot.astype(BF16)
+    name = iota((EXPERTS, tokens), 0)
+    named = (expert_ids[0:1, :] == name) | (expert_ids[1:2, :] == name)
+    named_f = named.astype(F32)
     before = (iota((tokens, tokens), 0) < iota((tokens, tokens), 1)).astype(F32).astype(BF16)
-    same = (iota((tokens, tokens), 0) == iota((tokens, tokens), 1)).astype(F32).astype(BF16)
+    rank = jnp.where(named, dot(named_f.astype(BF16), before), -1.0)
+    spot = (iota((EXPERTS, LANES), 0) == iota((EXPERTS, LANES), 1)).astype(F32).astype(BF16)
     turn = ((0,), (0,)), ((), ())
-    rank = lax.dot_general(hot_b, before, turn, preferred_element_type=F32)[0:EXPERTS]
-    is_hot = lax.dot_general(hot_b, same, turn, preferred_element_type=F32)[0:EXPERTS]
-    rank = jnp.where(is_hot > 0.5, rank, -1.0)
+    hot = lax.dot_general(named_f.astype(BF16), spot, turn, preferred_element_type=F32)
     slot = iota((MAIN, tokens), 0).astype(F32)
     picker = jnp.concatenate(
         [
@@ -223,7 +264,7 @@
     logits = (part[0] + part_in[0]) * scale
     chosen = logits * hot
     both = jnp.sum(chosen, axis=1, keepdims=True)
-    share = jnp.where(named, 1.0 / (1.0 + jnp.exp(both - 2.0 * chosen)), 0.0)
+    share = jnp.where(hot > 0.5, 1.0 / (1.0 + jnp.exp(both - 2.0 * chosen)), 0.0)
     high = share.astype(BF16).astype(F32)
     shares = (high + pltpu.roll(share - high, EXPERTS, 1)).astype(BF16)
     normed = (stream * scale * gain).astype(BF16)
@@ -337,7 +378,17 @@
         load.wait()
 
     columns = weights.shape[2]
-    tile = min(256, columns)
+    tile = min(1024, columns)
+
+    tiles = columns // tile
+
+    def tile_copy(block, index):
+        at = pl.ds(pl.multiple_of(index * tile, tile), tile)
+        return pltpu.make_async_copy(
+            hidden_out.at[block, :, at],
+            hidden_result.at[block, :, at],
+            hidden_sem.at[block * tiles + index],
+        )
 
     def block_rows(block, carry):
         share_rows = lined_up(block, rows_in, last_in, slice(half, half + LANES))
@@ -358,12 +409,37 @@
             hidden_out[block, :, at] = (gate / (1.0 + jnp.exp(-gate)) * up * slot_share).astype(
                 BF16
             )
+            tile_copy(block, index).start()
             return inner
 
         lax.fori_loop(0, columns // tile, one_tile, 0)
         return carry
 
     lax.fori_loop(0, width, block_rows, 0)
+
+    def settle(step, carry):
+        tile_copy(step // tiles, step % tiles).wait()
+        return carry
+
+    lax.fori_loop(0, width * tiles, settle, 0)
+    keep.wait()
+
+
+def pass_on(cuts, stream, hidden, stream_out, hidden_out, stream_in, hidden_in, ins, outs):
+    width = hidden.shape[2] // cuts
+    into = [pltpu.make_async_copy(stream, stream_in, ins.at[cuts])]
+    out = [pltpu.make_async_copy(stream_in, stream_out, outs.at[cuts])]
+    for cut in range(cuts):
+        at = (slice(None), slice(None), pl.ds(cut * width, width))
+        into.append(pltpu.make_async_copy(hidden.at[at], hidden_in.at[at], ins.at[cut]))
+        out.append(pltpu.make_async_copy(hidden_in.at[at], hidden_out.at[at], outs.at[cut]))
+    for copy in into:
+        copy.start()
+    for arrived, leaving in zip(into, out):
+        arrived.wait()
+        leaving.start()
+    for copy in out:
+        copy.wait()
 
 
 def shards(
@@ -382,10 +458,12 @@
     width = count // EXPERTS
     tokens, half = stream_in.shape
     columns = w_in.shape[2]
-    cache = paged_key_value_cache.reshape(2, -1, paged_key_value_cache.shape[-1])
+    cache = paged_key_value_cache
     w_chunks = 6
     rows = EXPERTS * CAP
-    vmem = pl.BlockSpec(memory_space=pltpu.VMEM)
+    hbm = pl.BlockSpec(memory_space=pl.ANY)
+    gain = norm_gain.reshape(1, -1)
+    near = (cache, queries, kv_new, stream_in, gain, w_router.T, expert_ids.T)
     smem = pl.BlockSpec(memory_space=pltpu.SMEM)
     dma = pltpu.SemaphoreType.DMA
     stream, hidden = pl.pallas_call(
@@ -395,9 +473,15 @@
             jax.ShapeDtypeStruct((tokens, half), BF16),
             jax.ShapeDtypeStruct((width, rows, columns), BF16),
         ),
-        in_specs=[smem, smem] + [vmem] * 7 + [pl.BlockSpec(memory_space=pl.ANY)],
-        out_specs=(vmem, vmem),
-        scratch_shapes=[
+        in_specs=[smem, smem] + [hbm] * 8,
+        out_specs=(hbm, hbm),
+        scratch_shapes=[pltpu.VMEM(array.shape, array.dtype) for array in near]
+        + [
+            pltpu.VMEM((tokens, half), BF16),
+            pltpu.VMEM((width, rows, columns), BF16),
+            dma((len(near),)),
+            dma,
+            dma((width * max(columns // 1024, 1),)),
             pltpu.VMEM(w_in.shape, BF16),
             pltpu.VMEM((count,) + cache.shape, BF16),
             pltpu.VMEM((2, tokens, LANES), F32),
@@ -417,20 +501,31 @@
         ]
         + [dma((count,))] * 8,
         compiler_params=pltpu.CompilerParams(
-            collective_id=0, has_side_effects=True, vmem_limit_bytes=67043328
+            collective_id=0, has_side_effects=True, vmem_limit_bytes=58 << 20
         ),
     )(
         page_table,
         prefix_len,
-        stream_in,
-        queries,
-        kv_new,
-        cache,
-        norm_gain.reshape(1, -1),
-        w_router,
-        expert_ids,
+        *near,
         w_in,
     )
+    cuts = 4 if columns % (4 * LANES) == 0 else 1
+    stream, hidden = pl.pallas_call(
+        lambda *refs: pass_on(cuts, *refs),
+        name="pass_on",
+        out_shape=(
+            jax.ShapeDtypeStruct(stream.shape, BF16),
+            jax.ShapeDtypeStruct(hidden.shape, BF16),
+        ),
+        in_specs=[hbm, hbm],
+        out_specs=(hbm, hbm),
+        scratch_shapes=[
+            pltpu.VMEM(stream.shape, BF16),
+            pltpu.VMEM(hidden.shape, BF16),
+            dma((cuts + 1,)),
+            dma((cuts + 1,)),
+        ],
+    )(stream, hidden)
     return stream, hidden.reshape(width * rows, columns)
 
 

time: 49.1 us -> 39.3 us (0.80)
  local copies, waits for them, and re-layouts: 8.61 us -> 0 us
  Pallas kernels: 38.9 us -> 37.7 us
    unnamed x4 -> x0, local copies, waits for them, and re-layouts: 7.29 us -> none
    pallas_call x1, Pallas kernels: 38.9 us -> 35.6 us  [shards(): pl.pallas_call(lambda *refs: kernel(count, w_chunks, paged_key_value_cach...]
    pallas_call x0 -> x1, Pallas kernels: none -> 2.13 us  [shards(): pl.pallas_call(lambda *refs: pass_on(cuts, *refs), name='pass_on', out_sh...]
    reshape x1 -> x0, local copies, waits for them, and re-layouts: 1.33 us -> none  [shards(): paged_key_value_cache.reshape(2, -1, paged_key_value_cache.shape[-1])]
where the time goes in v2:
time: 39.3 us; the launch traced here: 39 us
  Pallas kernels  37.7 us (96%)
  between operations  1.29 us (3%)
    pallas_call x1, Pallas kernels, shards(): pl.pallas_call(lambda *refs: kernel(count, w_chunks, paged_key_value_cach...  35.6 us
    pallas_call x1, Pallas kernels, shards(): pl.pallas_call(lambda *refs: pass_on(cuts, *refs), name='pass_on', out_sh...  2.13 us

profile of v2, /device:TPU:13, one launch (start us, length us, event | category | flops | bytes accessed | tf_op | source)
XLA Modules:
  0.0 39.0 jit_solution(13783351791050230293)
XLA Ops:
  1.3 35.6 %moe_prefill.1 = (bf16[64,1536]{1,0:T(8,128)(2,1)}, bf16[1,136,4096]{2,1,0:T(8,128)(2,1)}) custom-call(s32[1,8]{1,0:T(1,128)} %refs_0_.1, s32[1]{0:T(128)S(6)} %copy.12.refs_1_, bf16[2,2,4,512]{3,2,1,0:T(4,128)(2,1)} %refs_2_.1, bf16[64,1536]{1,0:T(8,128)(2,1)} %refs_3_.1, bf16[2,64,512]{2,1,0:T(8,128)(2,1)} %refs_4_.1, bf16[64,1536]{1,0:T(8,128)(2,1)} %refs_5_.1, ...), custom_call_target="tpu_custom_call" | custom-call | tf_op jit(solution)/shard_map/moe_prefill/pallas_call | solution.py:469
  36.9 2.1 %pass_on.1 = (bf16[64,1536]{1,0:T(8,128)(2,1)}, bf16[1,136,4096]{2,1,0:T(8,128)(2,1)}) custom-call(bf16[64,1536]{1,0:T(8,128)(2,1)} %get-tuple-element.6.refs_0_, bf16[1,136,4096]{2,1,0:T(8,128)(2,1)} %get-tuple-element.7.refs_1_), custom_call_target="tpu_custom_call" | custom-call | tf_op jit(solution)/shard_map/pass_on/pallas_call | solution.py:513
